TPU v7x, 32 devices: a whole 2x2x4 slice. The times are simulated.
32 devices in a mesh: grp: 2 (over y), var: 8 (over z, x), smp: 2 (over core).
Axes of the slice: x: 2, y: 2, z: 4, core: 2. Of those that a mesh axis runs over, the one named last changes fastest.
Arguments:
- genotypes: bfloat16 [15360, 1024], P(('grp', 'smp'), 'var'), parts along dimension 0, may hold values from 0 to 2, as said below
- ancestry_counts: int32 [15360, 32], P(('grp', 'smp')), parts along dimension 0, may hold values from 1 to 100
- residuals: int32 [15360, 16], P(('grp', 'smp')), parts along dimension 0, may hold values from -3000 to 3000
- freqs: float32 [64, 1024], P('grp', 'var'), parts along dimension 0, may hold values from 0.05 to 0.95
Outputs:
- q_new: float32 [15360, 32], P(('grp', 'smp', 'var')), parts along dimension 0
- q_gradient: float32 [15360, 32], P(('grp', 'smp', 'var')), parts along dimension 0
- p_new: float32 [64, 1024], P('grp', 'var'), parts along dimension 0
- p_gradient: float32 [64, 1024], P('grp', 'var'), parts along dimension 0
- z_score: float32 [64, 16, 1024], P('grp', None, 'var'), parts along dimension 0
There are 2 independent parts, one for each index of `grp`. A program takes and returns all parts, laid end to end along the dimension named above; each array names one. Nothing has to cross between parts.
Inputs may be any that keep to these rules, and one draw needn't show every extreme that they name: `genotypes`: dosages lie in the closed range from 0 to 2.
All inputs are finite; a program needn't handle non-finite values.
Results may differ from a plain program's by a relative error of at most 0.0003.
Values sent between devices are 32-bit elements; how exact they have to be, the bound alone decides.
A program may use at most 64 MiB of HBM per device.

v0:
```python
import functools
import math

import jax
import jax.numpy as jnp
from jax import lax
from jax.experimental import pallas as pl
from jax.experimental.pallas import tpu as pltpu
from jax.sharding import PartitionSpec as P

MESH = pl.DeviceIdType.MESH
F32 = jnp.float32
BF16 = jnp.bfloat16
LIMIT = 67043328 - 491520
MOST = 5


def normalize(fractions, gradient, second):
    weighted = fractions * (gradient + second[:, None])
    return weighted / jnp.sum(weighted, axis=1, keepdims=True)


def update_freqs(freqs, excess_sum, second_sum, sample_count):
    allele_sum = excess_sum + second_sum
    freq_next = freqs * allele_sum / (freqs * allele_sum + (1.0 - freqs) * second_sum)
    freq_gradient = excess_sum * freqs.shape[0] / math.sqrt(sample_count)
    return (freq_next, freq_gradient)


def shards_plain(genotypes, ancestry_counts, residuals, freqs):
    highest = lax.Precision.HIGHEST
    var_count = lax.axis_size("var")
    sample_rows = genotypes.shape[0]
    sample_count = sample_rows * lax.axis_size("smp")
    variant_count = genotypes.shape[1] * var_count
    anc_count = freqs.shape[0]
    trait_count = residuals.shape[1]
    counts = ancestry_counts.astype(jnp.float32)
    fractions = counts / jnp.sum(counts, axis=1, keepdims=True)
    dosage = genotypes.astype(jnp.float32)
    recon_rows = jnp.dot(fractions, freqs, precision=highest)
    ratio_a = dosage / recon_rows
    ratio_b = (2.0 - dosage) / (1.0 - recon_rows)
    excess = ratio_a - ratio_b
    gradient_part = jnp.dot(excess, freqs.T, precision=highest)
    second_part = jnp.sum(ratio_b, axis=1)
    excess_part = jnp.dot(fractions.T, excess, precision=highest)
    return_part = jnp.dot(fractions.T, ratio_b, precision=highest)
    share_rows = sample_rows // var_count
    first_row = lax.axis_index("var") * share_rows
    excess_sum, second_sum = lax.psum((excess_part, return_part), "smp")
    freq_next, freq_gradient = update_freqs(freqs, excess_sum, second_sum, sample_count)
    gradient_all, second_all = lax.psum((gradient_part, second_part), "var")
    fraction_next = normalize(fractions, gradient_all, second_all)
    own_next = lax.dynamic_slice_in_dim(fraction_next, first_row, share_rows, 0)
    own_gradient = lax.dynamic_slice_in_dim(gradient_all, first_row, share_rows, 0)
    scaled_gradient = own_gradient / math.sqrt(variant_count)
    ratio_next = dosage / jnp.dot(fraction_next, freqs, precision=highest)
    residual = residuals.astype(jnp.float32) / 1000.0
    trait_rows = (fraction_next[:, :, None] * residual[:, None, :]).reshape(
        sample_rows, anc_count * trait_count
    )
    score_part = jnp.dot(trait_rows.T, ratio_next, precision=highest)
    info_part = jnp.dot(
        (fraction_next * fraction_next).T, ratio_next * ratio_next, precision=highest
    )
    score_sum, info_sum = lax.psum((score_part, info_part), "smp")
    score_tiles = score_sum.reshape(anc_count, trait_count, genotypes.shape[1])
    z_score = score_tiles / jnp.sqrt(info_sum + 1e-06)[:, None, :]
    return (own_next, scaled_gradient, freq_next, freq_gradient, z_score)


def split(x):
    high = x.astype(BF16)
    return high, (x - high.astype(F32)).astype(BF16)


def dot(a, b):
    return jnp.dot(a, b, preferred_element_type=F32)


def dot_lanes(a, b):
    return lax.dot_general(a, b, (((1,), (1,)), ((), ())), preferred_element_type=F32)


def kernel(
    dims,
    geno_in, counts_in, resid_in, freqs_in,
    q_out, g_out, p_out, pg_out, z_out,
    geno, counts, resid, freqs, dos, qf, gf, fcol, frow, ebuf, tbuf,
    acc_ex, acc_sc, acc_in,
    xs, xr, zs, zr, go, gp, fs, fr, ss, sr,
    xs_s, xs_r, zs_s, zs_r, za_s, za_r, xa_s, xa_r, f_s, f_r, s_s, s_r, in_s,
):
    chunks, width, half, zs_n, rows, variant_count, sample_count, share, var_n = dims
    anc = freqs.shape[0]
    traits = resid.shape[0]
    mv = freqs.shape[1]
    me = lax.axis_index("var")
    core = lax.axis_index("smp")
    x = lax.rem(me, 2)
    z = me // 2
    partner = {"var": z * 2 + (1 - x)}
    twin = {"smp": 1 - core}
    z_peers = [{"var": lax.rem(z + d, zs_n) * 2 + x} for d in range(1, zs_n)]

    def load(src, dst, which, base=None, size=None):
        if base is not None:
            src, dst = src.at[pl.ds(base, size), :], dst.at[pl.ds(base, size), :]
        return pltpu.make_async_copy(src, dst, in_s.at[which])

    far_half = pl.multiple_of((1 - x) * half, 128)
    near_half = pl.multiple_of(x * half, 128)
    freqs_load = load(freqs_in, freqs, 0)
    counts_load = load(counts_in, counts, 1)
    far_load = load(geno_in, geno, 2, far_half, half)
    near_load = load(geno_in, geno, 3, near_half, half)
    resid_load = load(resid_in, resid, 4)
    for item in (freqs_load, counts_load, far_load, near_load, resid_load):
        item.start()

    barrier = pltpu.get_barrier_semaphore()
    for peer in [partner, twin] + z_peers:
        pl.semaphore_signal(barrier, inc=1, device_id=peer, device_id_type=MESH)

    freqs_load.wait()
    p = freqs[...]
    p_hi, p_lo = split(p)
    stack = jnp.concatenate([p_hi.astype(F32), p_lo.astype(F32)] * 2, axis=0)
    fcol[...] = stack.T.astype(BF16)
    frow[0:anc, 0:mv] = p_hi
    frow[0:anc, mv:] = p_hi
    frow[anc:, 0:mv] = p_lo
    frow[anc:, mv:] = p_lo
    acc_ex[...] = jnp.zeros_like(acc_ex)
    acc_sc[...] = jnp.zeros_like(acc_sc)
    acc_in[...] = jnp.zeros_like(acc_in)

    def lanes(which, c):
        return pl.multiple_of(which * half + c * width, 128)

    def first_pass(off):
        d = geno[pl.ds(off, width), :].astype(F32).T
        dos[:, pl.ds(off, width)] = d.astype(BF16)
        c = counts[:, pl.ds(off, width)].astype(F32)
        total = jnp.sum(c, axis=0, keepdims=True)
        cb = c.astype(BF16)
        none = jnp.zeros_like(cb)
        u = dot(fcol[...], jnp.concatenate([cb, cb, none, none], axis=0))
        w = total - u
        inverse = 1.0 / (u * w)
        b = (2.0 - d) * u * inverse
        e = d * w * inverse - b
        e_hi, e_lo = split(e)
        b_hi, b_lo = split(b)
        ebuf[0:mv, :] = e_hi
        ebuf[mv : 2 * mv, :] = e_lo
        ebuf[2 * mv : 3 * mv, :] = b_hi
        ebuf[3 * mv :, :] = b_lo
        g = dot(frow[...], ebuf[0 : 2 * mv, :])
        acc_ex[...] += dot_lanes(ebuf[...], jnp.concatenate([cb] * (128 // anc), axis=0))
        return (g[0:anc, :] + g[anc:, :]) * total

    def second_pass(off, g):
        c = counts[:, pl.ds(off, width)].astype(F32)
        f = c / jnp.sum(c, axis=0, keepdims=True)
        second = 2.0 * variant_count - jnp.sum(f * g, axis=0, keepdims=True)
        weighted = f * (g + second)
        q = weighted / jnp.sum(weighted, axis=0, keepdims=True)
        qf[:, pl.ds(off, width)] = q
        gf[:, pl.ds(off, width)] = g * (1.0 / math.sqrt(variant_count))
        q_hi, q_lo = split(q)
        recon = dot(fcol[...], jnp.concatenate([q_hi, q_hi, q_lo, q_lo], axis=0))
        r = dos[:, pl.ds(off, width)].astype(F32) / recon
        r_hi, r_lo = split(r)
        s_hi, s_lo = split(r * r)
        t = resid[:, pl.ds(off, width)].astype(F32)
        for k in range(anc):
            t_hi, t_lo = split(q[k : k + 1, :] * t)
            tbuf[traits * k : traits * (k + 1), 0:width] = t_hi
            tbuf[traits * k : traits * (k + 1), width:] = t_lo
        r_cat = jnp.concatenate([r_hi, r_lo], axis=0)
        acc_sc[...] += dot_lanes(tbuf[...], jnp.concatenate([r_cat, r_cat], axis=1))
        y_hi, y_lo = split(q * q)
        none = jnp.zeros_like(y_hi)
        acc_in[...] += dot_lanes(
            jnp.concatenate([s_hi, s_lo], axis=0),
            jnp.concatenate([y_hi, y_lo, none, none], axis=0),
        )

    def copy(src, dst, send, recv, peer):
        return pltpu.make_async_remote_copy(
            src_ref=src, dst_ref=dst, send_sem=send, recv_sem=recv, device_id=peer, device_id_type=MESH
        )

    def x_reduce(c):
        return copy(xs.at[c], xr.at[c], xs_s.at[c], xs_r.at[c], partner)

    def z_reduce(c, d):
        to = pl.multiple_of(lax.rem(z + d, zs_n) * rows, 8)
        return copy(
            zs.at[c, pl.ds(to, rows), :], zr.at[c, d - 1], zs_s.at[c, d - 1], zs_r.at[c, d - 1], z_peers[d - 1]
        )

    mine = pl.multiple_of(z * rows, 8)

    def z_gather(c, d):
        piece = go.at[c, pl.ds(mine, rows), :]
        return copy(piece, piece, za_s.at[c, d - 1], za_r.at[c, d - 1], z_peers[d - 1])

    def z_gathered(c, d):
        source = pl.multiple_of(lax.rem(z + zs_n - d, zs_n) * rows, 8)
        piece = go.at[c, pl.ds(source, rows), :]
        return copy(piece, piece, za_s.at[c, d - 1], za_r.at[c, d - 1], z_peers[d - 1])

    def x_gather(c):
        return copy(go.at[c], gp.at[c], xa_s.at[c], xa_r.at[c], partner)

    counts_load.wait()
    far_load.wait()
    xs[0] = first_pass(lanes(1 - x, 0))
    pl.semaphore_wait(barrier, 2 + len(z_peers))
    x_reduce(0).start()

    def step_far(c, carry):
        xs[c] = first_pass(lanes(1 - x, c))
        x_reduce(c).start()
        return carry

    lax.fori_loop(1, chunks, step_far, 0)
    near_load.wait()

    def step_near(c, carry):
        g = first_pass(lanes(x, c))
        x_reduce(c).wait_recv()
        zs[c] = g + xr[c]
        for d in range(1, zs_n):
            z_reduce(c, d).start()
        return carry

    lax.fori_loop(0, chunks, step_near, 0)

    ex = acc_ex[0:mv, :] + acc_ex[mv : 2 * mv, :]
    re = acc_ex[2 * mv : 3 * mv, :] + acc_ex[3 * mv :, :]
    fs[0:anc, :] = ex.T[0:anc, :]
    fs[anc:, :] = re.T[0:anc, :]
    freq_copy = copy(fs, fr, f_s, f_r, twin)
    freq_copy.start()

    def step_sum(c, carry):
        total = zs[c, pl.ds(mine, rows), :]
        for d in range(1, zs_n):
            z_reduce(c, d).wait_recv()
            total = total + zr[c, d - 1]
        go[c, pl.ds(mine, rows), :] = total
        for d in range(1, zs_n):
            z_gather(c, d).start()
        return carry

    lax.fori_loop(0, chunks, step_sum, 0)

    resid_load.wait()
    freq_copy.wait_recv()
    sums = fs[...] + fr[...]
    excess_sum = sums[0:anc, :]
    second_sum = sums[anc:, :]
    freq_next, freq_gradient = update_freqs(p, excess_sum, second_sum, sample_count)
    p_out[...] = freq_next
    pg_out[...] = freq_gradient

    def step_own(c, carry):
        for d in range(1, zs_n):
            z_gathered(c, d).wait_recv()
        x_gather(c).start()
        second_pass(lanes(x, c), go[c])
        return carry

    lax.fori_loop(0, chunks, step_own, 0)

    def step_other(c, carry):
        x_gather(c).wait_recv()
        second_pass(lanes(1 - x, c), gp[c])
        return carry

    lax.fori_loop(0, chunks, step_other, 0)

    tiles = anc * traits
    ss[0:tiles, :] = acc_sc[:, 0:mv] + acc_sc[:, mv:]
    info = (acc_in[0:mv, :] + acc_in[mv:, :]).T
    ss[tiles:, :] = info[0:anc, :] + info[anc : 2 * anc, :]
    score_copy = copy(ss, sr, s_s, s_r, twin)
    score_copy.start()

    for v in range(var_n):

        @pl.when(me == v)
        def _():
            q_out[...] = qf[:, share * v : share * (v + 1)]
            g_out[...] = gf[:, share * v : share * (v + 1)]

    def drain(c, carry):
        x_reduce(c).wait_send()
        x_gather(c).wait_send()
        for d in range(1, zs_n):
            z_reduce(c, d).wait_send()
            z_gather(c, d).wait_send()
        return carry

    lax.fori_loop(0, chunks, drain, 0)
    freq_copy.wait_send()
    score_copy.wait_recv()
    info_sum = ss[tiles:, :] + sr[tiles:, :]
    scale = 0.001 / jnp.sqrt(info_sum + 1e-06)
    for k in range(anc):
        at = slice(traits * k, traits * (k + 1))
        z_out[at, :] = (ss[at, :] + sr[at, :]) * scale[k : k + 1, :]
    score_copy.wait_send()


def store_kernel(*refs):
    count = len(refs) // 2
    sems = refs[-1]
    copies = [pltpu.make_async_copy(refs[i], refs[count + i], sems.at[i]) for i in range(count)]
    for item in copies:
        item.start()
    for item in copies:
        item.wait()


def store(*arrays):
    return pl.pallas_call(
        store_kernel,
        out_shape=tuple(jax.ShapeDtypeStruct(a.shape, a.dtype) for a in arrays),
        in_specs=[pl.BlockSpec(memory_space=pltpu.VMEM)] * len(arrays),
        out_specs=(pl.BlockSpec(memory_space=pl.ANY),) * len(arrays),
        scratch_shapes=[pltpu.SemaphoreType.DMA((len(arrays),))],
        compiler_params=pltpu.CompilerParams(vmem_limit_bytes=1024 * 1024),
        name="store",
    )(*arrays)


def fits(genotypes, residuals, freqs, var_n):
    samples, mv = genotypes.shape
    anc = freqs.shape[0]
    return (
        var_n == 8
        and lax.axis_size("smp") == 2
        and anc == 32
        and mv == 128
        and residuals.shape[1] % 16 == 0
        and samples % (2 * 128) == 0
        and samples % var_n == 0
    )


def shards(genotypes, ancestry_counts, residuals, freqs):
    var_n = lax.axis_size("var")
    if not fits(genotypes, residuals, freqs, var_n):
        return shards_plain(genotypes, ancestry_counts, residuals, freqs)
    samples, mv = genotypes.shape
    anc = freqs.shape[0]
    traits = residuals.shape[1]
    zs_n = var_n // 2
    rows = anc // zs_n
    half = samples // 2
    tiles = half // 128
    chunks = max(n for n in range(1, MOST + 1) if tiles % n == 0)
    width = half // chunks
    share = samples // var_n
    dims = (chunks, width, half, zs_n, rows, mv * var_n, samples * lax.axis_size("smp"), share, var_n)
    vmem = pl.BlockSpec(memory_space=pltpu.VMEM)
    dma = pltpu.SemaphoreType.DMA
    part = pltpu.VMEM((chunks, anc, width), F32)
    results = pl.pallas_call(
        functools.partial(kernel, dims),
        out_shape=(
            pltpu.VMEM((anc, share), F32),
            pltpu.VMEM((anc, share), F32),
            pltpu.VMEM((anc, mv), F32),
            pltpu.VMEM((anc, mv), F32),
            pltpu.VMEM((anc * traits, mv), F32),
        ),
        in_specs=[pl.BlockSpec(memory_space=pltpu.HBM)] * 4,
        out_specs=(vmem,) * 5,
        scratch_shapes=[
            pltpu.VMEM((samples, mv), BF16),
            pltpu.VMEM((anc, samples), jnp.int32),
            pltpu.VMEM((traits, samples), jnp.int32),
            pltpu.VMEM((anc, mv), F32),
            pltpu.VMEM((mv, samples), BF16),
            pltpu.VMEM((anc, samples), F32),
            pltpu.VMEM((anc, samples), F32),
            pltpu.VMEM((mv, 4 * anc), BF16),
            pltpu.VMEM((2 * anc, 2 * mv), BF16),
            pltpu.VMEM((4 * mv, width), BF16),
            pltpu.VMEM((anc * traits, 2 * width), BF16),
            pltpu.VMEM((4 * mv, 128), F32),
            pltpu.VMEM((anc * traits, 2 * mv), F32),
            pltpu.VMEM((2 * mv, 128), F32),
            part, part, part,
            pltpu.VMEM((chunks, zs_n - 1, rows, width), F32),
            part, part,
            pltpu.VMEM((2 * anc, mv), F32),
            pltpu.VMEM((2 * anc, mv), F32),
            pltpu.VMEM((anc * traits + anc, mv), F32),
            pltpu.VMEM((anc * traits + anc, mv), F32),
            dma((chunks,)), dma((chunks,)),
            dma((chunks, zs_n - 1)), dma((chunks, zs_n - 1)),
            dma((chunks, zs_n - 1)), dma((chunks, zs_n - 1)),
            dma((chunks,)), dma((chunks,)),
            dma, dma, dma, dma, dma((5,)),
        ],
        compiler_params=pltpu.CompilerParams(collective_id=0, has_side_effects=True, vmem_limit_bytes=LIMIT),
        name="em_step",
    )(genotypes, ancestry_counts.T, residuals.T, freqs)
    q_t, g_t, p_new, p_grad, z_flat = store(*results)
    return (q_t.T, g_t.T, p_new, p_grad, z_flat.reshape(anc, traits, mv))


def solution(mesh):
    in_specs = (
        P(("grp", "smp"), "var"),
        P(("grp", "smp"), None),
        P(("grp", "smp"), None),
        P("grp", "var"),
    )
    out_specs = (
        P(("grp", "smp", "var"), None),
        P(("grp", "smp", "var"), None),
        P("grp", "var"),
        P("grp", "var"),
        P("grp", None, "var"),
    )
    return jax.shard_map(shards, mesh=mesh, in_specs=in_specs, out_specs=out_specs, check_vma=False)
```

profile of v0, /device:TPU:0, one launch (start us, length us, event | category | flops | bytes accessed | tf_op | source)
XLA Modules:
  0.0 29.7 jit_solution(1178097710724333093)
XLA Ops:
  0.6 28.3 %em_step.1 = (f32[32,480]{1,0:T(8,128)S(1)}, f32[32,480]{1,0:T(8,128)S(1)}, f32[32,128]{1,0:T(8,128)S(1)}, f32[32,128]{1,0:T(8,128)S(1)}, f32[512,128]{1,0:T(8,128)S(1)}) custom-call(bf16[3840,128]{1,0:T(8,128)(2,1)} %geno_in.1, s32[32,3840]{1,0:T(8,128)} %bitcast.5, s32[16,3840]{1,0:T(8,128)} %bitcast.6, f32[32,128]{1,0:T(8,128)} %freqs_in.1), custom_call_target="tpu_custom_call" | custom-call | tf_op jit(solution)/shard_map/em_step/pallas_call | solution.py:374
  28.9 0.8 %store.1 = (f32[32,480]{1,0:T(8,128)}, f32[32,480]{1,0:T(8,128)}, f32[32,128]{1,0:T(8,128)}, f32[32,128]{1,0:T(8,128)}, f32[512,128]{1,0:T(8,128)}) custom-call(f32[32,480]{1,0:T(8,128)S(1)} %get-tuple-element.15.refs_0_, f32[32,480]{1,0:T(8,128)S(1)} %get-tuple-element.16.refs_1_, f32[32,128]{1,0:T(8,128)S(1)} %get-tuple-element.17.refs_2_, ...), custom_call_target="tpu_custom_call" | custom-call | tf_op jit(solution)/shard_map/store/pallas_call | solution.py:331
where the time goes:
time: 29.9 us; the launch traced here: 29.7 us
  Pallas kernels  29.1 us (97%)
  between operations  0.64 us (2%)
    pallas_call x1, Pallas kernels, shards(): pl.pallas_call(functools.partial(kernel, dims), out_shape=(pltpu.VMEM((an...  28.3 us
    pallas_call x1, Pallas kernels, store(): pl.pallas_call(store_kernel, out_shape=tuple((jax.ShapeDtypeStruct(a.shap...  0.8 us

commit v1 on v0

--- a/solution.py
+++ b/solution.py
@@ -13,6 +13,7 @@
 BF16 = jnp.bfloat16
 LIMIT = 67043328 - 491520
 MOST = 5
+LAG = 3
 
 
 def normalize(fractions, gradient, second):
@@ -89,10 +90,11 @@
     q_out, g_out, p_out, pg_out, z_out,
     geno, counts, resid, freqs, dos, qf, gf, fcol, frow, ebuf, tbuf,
     acc_ex, acc_sc, acc_in,
-    xs, xr, zs, zr, go, gp, fs, fr, ss, sr,
-    xs_s, xs_r, zs_s, zs_r, za_s, za_r, xa_s, xa_r, f_s, f_r, s_s, s_r, in_s,
+    xs, xr, zs, er, mr, go, gp, fs, fr, ss, sr,
+    xs_s, xs_r, e_s, e_r, m_s, m_r, o_s, o_r, xa_s, xa_r, f_s, f_r, s_s, s_r, in_s,
 ):
-    chunks, width, half, zs_n, rows, variant_count, sample_count, share, var_n = dims
+    chunks, width, half, variant_count, sample_count, share, var_n = dims
+    sub = width // 128
     anc = freqs.shape[0]
     traits = resid.shape[0]
     mv = freqs.shape[1]
@@ -100,28 +102,53 @@
     core = lax.axis_index("smp")
     x = lax.rem(me, 2)
     z = me // 2
+    zn = z + 1 - 2 * lax.rem(z, 2)
+    middle = jnp.logical_or(z == 1, z == 2)
+    end = jnp.logical_or(z == 0, z == 3)
     partner = {"var": z * 2 + (1 - x)}
     twin = {"smp": 1 - core}
-    z_peers = [{"var": lax.rem(z + d, zs_n) * 2 + x} for d in range(1, zs_n)]
+    beside = {"var": zn * 2 + x}
+    across = {"var": lax.rem(7 - z, 4) * 2 + x}
 
     def load(src, dst, which, base=None, size=None):
         if base is not None:
             src, dst = src.at[pl.ds(base, size), :], dst.at[pl.ds(base, size), :]
         return pltpu.make_async_copy(src, dst, in_s.at[which])
 
+    def load_lanes(src, dst, which, base, size):
+        return pltpu.make_async_copy(
+            src.at[:, pl.ds(base, size)], dst.at[:, pl.ds(base, size)], in_s.at[which]
+        )
+
     far_half = pl.multiple_of((1 - x) * half, 128)
     near_half = pl.multiple_of(x * half, 128)
     freqs_load = load(freqs_in, freqs, 0)
-    counts_load = load(counts_in, counts, 1)
-    far_load = load(geno_in, geno, 2, far_half, half)
-    near_load = load(geno_in, geno, 3, near_half, half)
-    resid_load = load(resid_in, resid, 4)
-    for item in (freqs_load, counts_load, far_load, near_load, resid_load):
+    first_loads = (
+        load_lanes(counts_in, counts, 1, far_half, width),
+        load(geno_in, geno, 2, far_half, width),
+    )
+    later_loads = ()
+    if chunks > 1:
+        far_next = pl.multiple_of(far_half + width, 128)
+        later_loads = (
+            load_lanes(counts_in, counts, 3, far_next, half - width),
+            load(geno_in, geno, 4, far_next, half - width),
+        )
+    near_loads = (
+        load_lanes(counts_in, counts, 5, near_half, half),
+        load(geno_in, geno, 6, near_half, half),
+    )
+    resid_load = load(resid_in, resid, 7)
+    for item in (freqs_load,) + first_loads + later_loads + near_loads + (resid_load,):
         item.start()
 
     barrier = pltpu.get_barrier_semaphore()
-    for peer in [partner, twin] + z_peers:
+    for peer in (partner, twin, beside):
         pl.semaphore_signal(barrier, inc=1, device_id=peer, device_id_type=MESH)
+
+    @pl.when(middle)
+    def _():
+        pl.semaphore_signal(barrier, inc=1, device_id=across, device_id_type=MESH)
 
     freqs_load.wait()
     p = freqs[...]
@@ -193,49 +220,81 @@
             src_ref=src, dst_ref=dst, send_sem=send, recv_sem=recv, device_id=peer, device_id_type=MESH
         )
 
-    def x_reduce(c):
-        return copy(xs.at[c], xr.at[c], xs_s.at[c], xs_r.at[c], partner)
-
-    def z_reduce(c, d):
-        to = pl.multiple_of(lax.rem(z + d, zs_n) * rows, 8)
-        return copy(
-            zs.at[c, pl.ds(to, rows), :], zr.at[c, d - 1], zs_s.at[c, d - 1], zs_r.at[c, d - 1], z_peers[d - 1]
-        )
-
-    mine = pl.multiple_of(z * rows, 8)
-
-    def z_gather(c, d):
-        piece = go.at[c, pl.ds(mine, rows), :]
-        return copy(piece, piece, za_s.at[c, d - 1], za_r.at[c, d - 1], z_peers[d - 1])
-
-    def z_gathered(c, d):
-        source = pl.multiple_of(lax.rem(z + zs_n - d, zs_n) * rows, 8)
-        piece = go.at[c, pl.ds(source, rows), :]
-        return copy(piece, piece, za_s.at[c, d - 1], za_r.at[c, d - 1], z_peers[d - 1])
-
-    def x_gather(c):
-        return copy(go.at[c], gp.at[c], xa_s.at[c], xa_r.at[c], partner)
-
-    counts_load.wait()
-    far_load.wait()
-    xs[0] = first_pass(lanes(1 - x, 0))
-    pl.semaphore_wait(barrier, 2 + len(z_peers))
-    x_reduce(0).start()
+    def x_reduce(t):
+        return copy(xs.at[t], xr.at[t], xs_s.at[t], xs_r.at[t], partner)
+
+    def inward(t):
+        return copy(zs.at[t], er.at[t], e_s.at[t], e_r.at[t], beside)
+
+    def exchange(t):
+        return copy(zs.at[t], mr.at[t], m_s.at[t], m_r.at[t], across)
+
+    def outward(t):
+        return copy(go.at[t], go.at[t], o_s.at[t], o_r.at[t], beside)
+
+    def x_gather(t):
+        return copy(go.at[t], gp.at[t], xa_s.at[t], xa_r.at[t], partner)
+
+    def put(ref, c, g):
+        for j in range(sub):
+            ref[c * sub + j] = g[:, 128 * j : 128 * (j + 1)]
+
+    def take(ref, c):
+        return jnp.concatenate([ref[c * sub + j] for j in range(sub)], axis=1)
+
+    for item in first_loads:
+        item.wait()
+    put(xs, 0, first_pass(lanes(1 - x, 0)))
+
+    @pl.when(middle)
+    def _():
+        pl.semaphore_wait(barrier, 4)
+
+    @pl.when(end)
+    def _():
+        pl.semaphore_wait(barrier, 3)
+
+    for j in range(sub):
+        x_reduce(j).start()
+    for item in later_loads:
+        item.wait()
 
     def step_far(c, carry):
-        xs[c] = first_pass(lanes(1 - x, c))
-        x_reduce(c).start()
+        put(xs, c, first_pass(lanes(1 - x, c)))
+        for j in range(sub):
+            x_reduce(c * sub + j).start()
         return carry
 
     lax.fori_loop(1, chunks, step_far, 0)
-    near_load.wait()
+    for item in near_loads:
+        item.wait()
+
+    def add_inward(t):
+        inward(t).wait_recv()
+        zs[t] = zs[t] + er[t]
+        exchange(t).start()
+
+    def add_exchange(t):
+        exchange(t).wait_recv()
+        go[t] = zs[t] + mr[t]
+        outward(t).start()
+        x_gather(t).start()
 
     def step_near(c, carry):
-        g = first_pass(lanes(x, c))
-        x_reduce(c).wait_recv()
-        zs[c] = g + xr[c]
-        for d in range(1, zs_n):
-            z_reduce(c, d).start()
+        put(zs, c, first_pass(lanes(x, c)))
+        for j in range(sub):
+            t = c * sub + j
+            x_reduce(t).wait_recv()
+            zs[t] = zs[t] + xr[t]
+
+            @pl.when(end)
+            def _(t=t):
+                inward(t).start()
+
+            @pl.when(jnp.logical_and(middle, c >= LAG))
+            def _(t=t):
+                add_inward(t - LAG * sub)
+
         return carry
 
     lax.fori_loop(0, chunks, step_near, 0)
@@ -247,39 +306,42 @@
     freq_copy = copy(fs, fr, f_s, f_r, twin)
     freq_copy.start()
 
-    def step_sum(c, carry):
-        total = zs[c, pl.ds(mine, rows), :]
-        for d in range(1, zs_n):
-            z_reduce(c, d).wait_recv()
-            total = total + zr[c, d - 1]
-        go[c, pl.ds(mine, rows), :] = total
-        for d in range(1, zs_n):
-            z_gather(c, d).start()
+    @pl.when(middle)
+    def _():
+        def step_inward(t, carry):
+            add_inward(t)
+            return carry
+
+        lax.fori_loop(max(0, chunks - LAG) * sub, min(LAG, chunks) * sub, step_inward, 0)
+
+    resid_load.wait()
+
+    def step_own(c, carry):
+        for j in range(sub):
+            t = c * sub + j
+
+            @pl.when(jnp.logical_and(middle, c + LAG < chunks))
+            def _(t=t):
+                add_inward(t + LAG * sub)
+
+            @pl.when(middle)
+            def _(t=t):
+                add_exchange(t)
+
+            @pl.when(end)
+            def _(t=t):
+                outward(t).wait_recv()
+                x_gather(t).start()
+
+        second_pass(lanes(x, c), take(go, c))
         return carry
 
-    lax.fori_loop(0, chunks, step_sum, 0)
-
-    resid_load.wait()
-    freq_copy.wait_recv()
-    sums = fs[...] + fr[...]
-    excess_sum = sums[0:anc, :]
-    second_sum = sums[anc:, :]
-    freq_next, freq_gradient = update_freqs(p, excess_sum, second_sum, sample_count)
-    p_out[...] = freq_next
-    pg_out[...] = freq_gradient
-
-    def step_own(c, carry):
-        for d in range(1, zs_n):
-            z_gathered(c, d).wait_recv()
-        x_gather(c).start()
-        second_pass(lanes(x, c), go[c])
-        return carry
-
     lax.fori_loop(0, chunks, step_own, 0)
 
     def step_other(c, carry):
-        x_gather(c).wait_recv()
-        second_pass(lanes(1 - x, c), gp[c])
+        for j in range(sub):
+            x_gather(c * sub + j).wait_recv()
+        second_pass(lanes(1 - x, c), take(gp, c))
         return carry
 
     lax.fori_loop(0, chunks, step_other, 0)
@@ -291,6 +353,14 @@
     score_copy = copy(ss, sr, s_s, s_r, twin)
     score_copy.start()
 
+    freq_copy.wait_recv()
+    sums = fs[...] + fr[...]
+    excess_sum = sums[0:anc, :]
+    second_sum = sums[anc:, :]
+    freq_next, freq_gradient = update_freqs(freqs[...], excess_sum, second_sum, sample_count)
+    p_out[...] = freq_next
+    pg_out[...] = freq_gradient
+
     for v in range(var_n):
 
         @pl.when(me == v)
@@ -298,15 +368,22 @@
             q_out[...] = qf[:, share * v : share * (v + 1)]
             g_out[...] = gf[:, share * v : share * (v + 1)]
 
-    def drain(c, carry):
-        x_reduce(c).wait_send()
-        x_gather(c).wait_send()
-        for d in range(1, zs_n):
-            z_reduce(c, d).wait_send()
-            z_gather(c, d).wait_send()
+    def drain(t, carry):
+        x_reduce(t).wait_send()
+        x_gather(t).wait_send()
+
+        @pl.when(end)
+        def _():
+            inward(t).wait_send()
+
+        @pl.when(middle)
+        def _():
+            exchange(t).wait_send()
+            outward(t).wait_send()
+
         return carry
 
-    lax.fori_loop(0, chunks, drain, 0)
+    lax.fori_loop(0, chunks * sub, drain, 0)
     freq_copy.wait_send()
     score_copy.wait_recv()
     info_sum = ss[tiles:, :] + sr[tiles:, :]
@@ -360,17 +437,16 @@
     samples, mv = genotypes.shape
     anc = freqs.shape[0]
     traits = residuals.shape[1]
-    zs_n = var_n // 2
-    rows = anc // zs_n
     half = samples // 2
     tiles = half // 128
     chunks = max(n for n in range(1, MOST + 1) if tiles % n == 0)
     width = half // chunks
     share = samples // var_n
-    dims = (chunks, width, half, zs_n, rows, mv * var_n, samples * lax.axis_size("smp"), share, var_n)
+    dims = (chunks, width, half, mv * var_n, samples * lax.axis_size("smp"), share, var_n)
     vmem = pl.BlockSpec(memory_space=pltpu.VMEM)
     dma = pltpu.SemaphoreType.DMA
-    part = pltpu.VMEM((chunks, anc, width), F32)
+    part = pltpu.VMEM((half // 128, anc, 128), F32)
+    flags = dma((half // 128,))
     results = pl.pallas_call(
         functools.partial(kernel, dims),
         out_shape=(
@@ -397,18 +473,13 @@
             pltpu.VMEM((4 * mv, 128), F32),
             pltpu.VMEM((anc * traits, 2 * mv), F32),
             pltpu.VMEM((2 * mv, 128), F32),
-            part, part, part,
-            pltpu.VMEM((chunks, zs_n - 1, rows, width), F32),
-            part, part,
+            part, part, part, part, part, part, part,
             pltpu.VMEM((2 * anc, mv), F32),
             pltpu.VMEM((2 * anc, mv), F32),
             pltpu.VMEM((anc * traits + anc, mv), F32),
             pltpu.VMEM((anc * traits + anc, mv), F32),
-            dma((chunks,)), dma((chunks,)),
-            dma((chunks, zs_n - 1)), dma((chunks, zs_n - 1)),
-            dma((chunks, zs_n - 1)), dma((chunks, zs_n - 1)),
-            dma((chunks,)), dma((chunks,)),
-            dma, dma, dma, dma, dma((5,)),
+            flags, flags, flags, flags, flags, flags, flags, flags, flags, flags,
+            dma, dma, dma, dma, dma((8,)),
         ],
         compiler_params=pltpu.CompilerParams(collective_id=0, has_side_effects=True, vmem_limit_bytes=LIMIT),
         name="em_step",

time: 29.9 us -> 29.4 us (0.983)
  Pallas kernels: 29.1 us -> 28.5 us
    pallas_call x1, Pallas kernels: 28.3 us -> 27.7 us  [shards(): pl.pallas_call(functools.partial(kernel, dims), out_shape=(pltpu.VMEM((an...]
where the time goes in v1:
time: 29.4 us; the launch traced here: 29.2 us
  Pallas kernels  28.5 us (97%)
  between operations  0.64 us (2%)
    pallas_call x1, Pallas kernels, shards(): pl.pallas_call(functools.partial(kernel, dims), out_shape=(pltpu.VMEM((an...  27.7 us
    pallas_call x1, Pallas kernels, store(): pl.pallas_call(store_kernel, out_shape=tuple((jax.ShapeDtypeStruct(a.shap...  0.8 us

profile of v1, /device:TPU:0, one launch (start us, length us, event | category | flops | bytes accessed | tf_op | source)
XLA Modules:
  0.0 29.2 jit_solution(10429427750435606032)
XLA Ops:
  0.6 27.7 %em_step.1 = (f32[32,480]{1,0:T(8,128)S(1)}, f32[32,480]{1,0:T(8,128)S(1)}, f32[32,128]{1,0:T(8,128)S(1)}, f32[32,128]{1,0:T(8,128)S(1)}, f32[512,128]{1,0:T(8,128)S(1)}) custom-call(bf16[3840,128]{1,0:T(8,128)(2,1)} %geno_in.1, s32[32,3840]{1,0:T(8,128)} %bitcast.5, s32[16,3840]{1,0:T(8,128)} %bitcast.6, f32[32,128]{1,0:T(8,128)} %freqs_in.1), custom_call_target="tpu_custom_call" | custom-call | tf_op jit(solution)/shard_map/em_step/pallas_call | solution.py:450
  28.4 0.8 %store.1 = (f32[32,480]{1,0:T(8,128)}, f32[32,480]{1,0:T(8,128)}, f32[32,128]{1,0:T(8,128)}, f32[32,128]{1,0:T(8,128)}, f32[512,128]{1,0:T(8,128)}) custom-call(f32[32,480]{1,0:T(8,128)S(1)} %get-tuple-element.15.refs_0_, f32[32,480]{1,0:T(8,128)S(1)} %get-tuple-element.16.refs_1_, f32[32,128]{1,0:T(8,128)S(1)} %get-tuple-element.17.refs_2_, ...), custom_call_target="tpu_custom_call" | custom-call | tf_op jit(solution)/shard_map/store/pallas_call | solution.py:408

commit v2 on v1

--- a/solution.py
+++ b/solution.py
@@ -91,7 +91,7 @@
     geno, counts, resid, freqs, dos, qf, gf, fcol, frow, ebuf, tbuf,
     acc_ex, acc_sc, acc_in,
     xs, xr, zs, er, mr, go, gp, fs, fr, ss, sr,
-    xs_s, xs_r, e_s, e_r, m_s, m_r, o_s, o_r, xa_s, xa_r, f_s, f_r, s_s, s_r, in_s,
+    xs_s, xs_r, z_s, z_r, m_s, m_r, xa_s, xa_r, f_s, f_r, s_s, s_r, in_s,
 ):
     chunks, width, half, variant_count, sample_count, share, var_n = dims
     sub = width // 128
@@ -202,17 +202,20 @@
         r_hi, r_lo = split(r)
         s_hi, s_lo = split(r * r)
         t = resid[:, pl.ds(off, width)].astype(F32)
-        for k in range(anc):
-            t_hi, t_lo = split(q[k : k + 1, :] * t)
-            tbuf[traits * k : traits * (k + 1), 0:width] = t_hi
-            tbuf[traits * k : traits * (k + 1), width:] = t_lo
         r_cat = jnp.concatenate([r_hi, r_lo], axis=0)
-        acc_sc[...] += dot_lanes(tbuf[...], jnp.concatenate([r_cat, r_cat], axis=1))
+        r_cat = jnp.concatenate([r_cat, r_cat], axis=1)
+        step = anc // 2
+        for m in range(2):
+            for k in range(step * m, step * (m + 1)):
+                t_hi, t_lo = split(q[k : k + 1, :] * t)
+                tbuf[traits * k : traits * (k + 1), 0:width] = t_hi
+                tbuf[traits * k : traits * (k + 1), width:] = t_lo
+            at = slice(traits * step * m, traits * step * (m + 1))
+            acc_sc[at, :] += dot_lanes(tbuf[at, :], r_cat)
         y_hi, y_lo = split(q * q)
         none = jnp.zeros_like(y_hi)
         acc_in[...] += dot_lanes(
-            jnp.concatenate([s_hi, s_lo], axis=0),
-            jnp.concatenate([y_hi, y_lo, none, none], axis=0),
+            jnp.concatenate([y_hi, y_lo], axis=0), jnp.concatenate([s_hi, s_lo], axis=0)
         )
 
     def copy(src, dst, send, recv, peer):
@@ -221,19 +224,23 @@
         )
 
     def x_reduce(t):
-        return copy(xs.at[t], xr.at[t], xs_s.at[t], xs_r.at[t], partner)
+        return copy(xs.at[t], xr.at[t], xs_s, xs_r.at[t], partner)
 
     def inward(t):
-        return copy(zs.at[t], er.at[t], e_s.at[t], e_r.at[t], beside)
+        return copy(zs.at[t], er.at[t], z_s, z_r.at[t], beside)
 
     def exchange(t):
-        return copy(zs.at[t], mr.at[t], m_s.at[t], m_r.at[t], across)
+        return copy(zs.at[t], mr.at[t], m_s, m_r.at[t], across)
 
     def outward(t):
-        return copy(go.at[t], go.at[t], o_s.at[t], o_r.at[t], beside)
-
-    def x_gather(t):
-        return copy(go.at[t], gp.at[t], xa_s.at[t], xa_r.at[t], partner)
+        return copy(go.at[t], go.at[t], z_s, z_r.at[t], beside)
+
+    def x_gather(c, j):
+        return copy(go.at[c * sub + j], gp.at[c * sub + j], xa_s, xa_r.at[c], partner)
+
+    def x_gathered(c):
+        at = pl.ds(c * sub, sub)
+        return copy(go.at[at], gp.at[at], xa_s, xa_r.at[c], partner)
 
     def put(ref, c, g):
         for j in range(sub):
@@ -274,11 +281,12 @@
         zs[t] = zs[t] + er[t]
         exchange(t).start()
 
-    def add_exchange(t):
+    def add_exchange(c, j):
+        t = c * sub + j
         exchange(t).wait_recv()
         go[t] = zs[t] + mr[t]
         outward(t).start()
-        x_gather(t).start()
+        x_gather(c, j).start()
 
     def step_near(c, carry):
         put(zs, c, first_pass(lanes(x, c)))
@@ -312,7 +320,19 @@
             add_inward(t)
             return carry
 
+        def step_exchange(c, carry):
+            for j in range(sub):
+                t = c * sub + j
+
+                @pl.when(c + LAG < chunks)
+                def _(t=t):
+                    add_inward(t + LAG * sub)
+
+                add_exchange(c, j)
+            return carry
+
         lax.fori_loop(max(0, chunks - LAG) * sub, min(LAG, chunks) * sub, step_inward, 0)
+        lax.fori_loop(0, chunks, step_exchange, 0)
 
     resid_load.wait()
 
@@ -320,18 +340,10 @@
         for j in range(sub):
             t = c * sub + j
 
-            @pl.when(jnp.logical_and(middle, c + LAG < chunks))
-            def _(t=t):
-                add_inward(t + LAG * sub)
-
-            @pl.when(middle)
-            def _(t=t):
-                add_exchange(t)
-
             @pl.when(end)
-            def _(t=t):
+            def _(t=t, j=j):
                 outward(t).wait_recv()
-                x_gather(t).start()
+                x_gather(c, j).start()
 
         second_pass(lanes(x, c), take(go, c))
         return carry
@@ -339,8 +351,7 @@
     lax.fori_loop(0, chunks, step_own, 0)
 
     def step_other(c, carry):
-        for j in range(sub):
-            x_gather(c * sub + j).wait_recv()
+        x_gathered(c).wait_recv()
         second_pass(lanes(1 - x, c), take(gp, c))
         return carry
 
@@ -348,8 +359,8 @@
 
     tiles = anc * traits
     ss[0:tiles, :] = acc_sc[:, 0:mv] + acc_sc[:, mv:]
-    info = (acc_in[0:mv, :] + acc_in[mv:, :]).T
-    ss[tiles:, :] = info[0:anc, :] + info[anc : 2 * anc, :]
+    info = acc_in[0:anc, :] + acc_in[anc:, :]
+    ss[tiles:, :] = info[:, 0:mv] + info[:, mv:]
     score_copy = copy(ss, sr, s_s, s_r, twin)
     score_copy.start()
 
@@ -368,22 +379,14 @@
             q_out[...] = qf[:, share * v : share * (v + 1)]
             g_out[...] = gf[:, share * v : share * (v + 1)]
 
-    def drain(t, carry):
-        x_reduce(t).wait_send()
-        x_gather(t).wait_send()
-
-        @pl.when(end)
-        def _():
-            inward(t).wait_send()
-
-        @pl.when(middle)
-        def _():
-            exchange(t).wait_send()
-            outward(t).wait_send()
-
-        return carry
-
-    lax.fori_loop(0, chunks * sub, drain, 0)
+    copy(xs, xr, xs_s, xs_r.at[0], partner).wait_send()
+    copy(go, gp, xa_s, xa_r.at[0], partner).wait_send()
+    copy(zs, er, z_s, z_r.at[0], beside).wait_send()
+
+    @pl.when(middle)
+    def _():
+        copy(zs, mr, m_s, m_r.at[0], across).wait_send()
+
     freq_copy.wait_send()
     score_copy.wait_recv()
     info_sum = ss[tiles:, :] + sr[tiles:, :]
@@ -472,13 +475,13 @@
             pltpu.VMEM((anc * traits, 2 * width), BF16),
             pltpu.VMEM((4 * mv, 128), F32),
             pltpu.VMEM((anc * traits, 2 * mv), F32),
-            pltpu.VMEM((2 * mv, 128), F32),
+            pltpu.VMEM((2 * anc, 2 * mv), F32),
             part, part, part, part, part, part, part,
             pltpu.VMEM((2 * anc, mv), F32),
             pltpu.VMEM((2 * anc, mv), F32),
             pltpu.VMEM((anc * traits + anc, mv), F32),
             pltpu.VMEM((anc * traits + anc, mv), F32),
-            flags, flags, flags, flags, flags, flags, flags, flags, flags, flags,
+            dma, flags, dma, flags, dma, flags, dma, dma((chunks,)),
             dma, dma, dma, dma, dma((8,)),
         ],
         compiler_params=pltpu.CompilerParams(collective_id=0, has_side_effects=True, vmem_limit_bytes=LIMIT),

time: 29.4 us -> 27.9 us (0.949)
  Pallas kernels: 28.5 us -> 27.1 us
    pallas_call x1, Pallas kernels: 27.7 us -> 26.3 us  [shards(): pl.pallas_call(functools.partial(kernel, dims), out_shape=(pltpu.VMEM((an...]
where the time goes in v2:
time: 27.9 us; the launch traced here: 27.7 us
  Pallas kernels  27.1 us (97%)
  between operations  0.64 us (2%)
    pallas_call x1, Pallas kernels, shards(): pl.pallas_call(functools.partial(kernel, dims), out_shape=(pltpu.VMEM((an...  26.3 us
    pallas_call x1, Pallas kernels, store(): pl.pallas_call(store_kernel, out_shape=tuple((jax.ShapeDtypeStruct(a.shap...  0.8 us

profile of v2, /device:TPU:0, one launch (start us, length us, event | category | flops | bytes accessed | tf_op | source)
XLA Modules:
  0.0 27.7 jit_solution(11297928161488696030)
XLA Ops:
  0.6 26.3 %em_step.1 = (f32[32,480]{1,0:T(8,128)S(1)}, f32[32,480]{1,0:T(8,128)S(1)}, f32[32,128]{1,0:T(8,128)S(1)}, f32[32,128]{1,0:T(8,128)S(1)}, f32[512,128]{1,0:T(8,128)S(1)}) custom-call(bf16[3840,128]{1,0:T(8,128)(2,1)} %geno_in.1, s32[32,3840]{1,0:T(8,128)} %bitcast.5, s32[16,3840]{1,0:T(8,128)} %bitcast.6, f32[32,128]{1,0:T(8,128)} %freqs_in.1), custom_call_target="tpu_custom_call" | custom-call | tf_op jit(solution)/shard_map/em_step/pallas_call | solution.py:453
  26.9 0.8 %store.1 = (f32[32,480]{1,0:T(8,128)}, f32[32,480]{1,0:T(8,128)}, f32[32,128]{1,0:T(8,128)}, f32[32,128]{1,0:T(8,128)}, f32[512,128]{1,0:T(8,128)}) custom-call(f32[32,480]{1,0:T(8,128)S(1)} %get-tuple-element.15.refs_0_, f32[32,480]{1,0:T(8,128)S(1)} %get-tuple-element.16.refs_1_, f32[32,128]{1,0:T(8,128)S(1)} %get-tuple-element.17.refs_2_, ...), custom_call_target="tpu_custom_call" | custom-call | tf_op jit(solution)/shard_map/store/pallas_call | solution.py:411

commit v3 on v2

--- a/solution.py
+++ b/solution.py
@@ -13,6 +13,9 @@
 BF16 = jnp.bfloat16
 LIMIT = 67043328 - 491520
 MOST = 5
+NEAR_LAG = 3
+OWN = 3
+OTHER = 5
 LAG = 3
 
 
@@ -88,12 +91,12 @@
     dims,
     geno_in, counts_in, resid_in, freqs_in,
     q_out, g_out, p_out, pg_out, z_out,
-    geno, counts, resid, freqs, dos, qf, gf, fcol, frow, ebuf, tbuf,
+    geno, counts, resid, freqs, fstack, qf, gf, fcol, frow, ebuf, tbuf,
     acc_ex, acc_sc, acc_in,
     xs, xr, zs, er, mr, go, gp, fs, fr, ss, sr,
     xs_s, xs_r, z_s, z_r, m_s, m_r, xa_s, xa_r, f_s, f_r, s_s, s_r, in_s,
 ):
-    chunks, width, half, variant_count, sample_count, share, var_n = dims
+    chunks, width, half, own_per, per, variant_count, sample_count, share, var_n = dims
     sub = width // 128
     anc = freqs.shape[0]
     traits = resid.shape[0]
@@ -150,25 +153,25 @@
     def _():
         pl.semaphore_signal(barrier, inc=1, device_id=across, device_id_type=MESH)
 
+    acc_ex[...] = jnp.zeros_like(acc_ex)
+    acc_sc[...] = jnp.zeros_like(acc_sc)
+    acc_in[...] = jnp.zeros_like(acc_in)
     freqs_load.wait()
     p = freqs[...]
     p_hi, p_lo = split(p)
     stack = jnp.concatenate([p_hi.astype(F32), p_lo.astype(F32)] * 2, axis=0)
     fcol[...] = stack.T.astype(BF16)
+    fstack[...] = stack.astype(BF16)
     frow[0:anc, 0:mv] = p_hi
     frow[0:anc, mv:] = p_hi
     frow[anc:, 0:mv] = p_lo
     frow[anc:, mv:] = p_lo
-    acc_ex[...] = jnp.zeros_like(acc_ex)
-    acc_sc[...] = jnp.zeros_like(acc_sc)
-    acc_in[...] = jnp.zeros_like(acc_in)
 
     def lanes(which, c):
         return pl.multiple_of(which * half + c * width, 128)
 
     def first_pass(off):
         d = geno[pl.ds(off, width), :].astype(F32).T
-        dos[:, pl.ds(off, width)] = d.astype(BF16)
         c = counts[:, pl.ds(off, width)].astype(F32)
         total = jnp.sum(c, axis=0, keepdims=True)
         cb = c.astype(BF16)
@@ -189,6 +192,7 @@
         return (g[0:anc, :] + g[anc:, :]) * total
 
     def second_pass(off, g):
+        width = g.shape[1]
         c = counts[:, pl.ds(off, width)].astype(F32)
         f = c / jnp.sum(c, axis=0, keepdims=True)
         second = 2.0 * variant_count - jnp.sum(f * g, axis=0, keepdims=True)
@@ -197,25 +201,31 @@
         qf[:, pl.ds(off, width)] = q
         gf[:, pl.ds(off, width)] = g * (1.0 / math.sqrt(variant_count))
         q_hi, q_lo = split(q)
-        recon = dot(fcol[...], jnp.concatenate([q_hi, q_hi, q_lo, q_lo], axis=0))
-        r = dos[:, pl.ds(off, width)].astype(F32) / recon
+        recon = lax.dot_general(
+            jnp.concatenate([q_hi, q_hi, q_lo, q_lo], axis=0),
+            fstack[...],
+            (((0,), (0,)), ((), ())),
+            preferred_element_type=F32,
+        )
+        r = geno[pl.ds(off, width), :].astype(F32) / recon
         r_hi, r_lo = split(r)
         s_hi, s_lo = split(r * r)
         t = resid[:, pl.ds(off, width)].astype(F32)
-        r_cat = jnp.concatenate([r_hi, r_lo], axis=0)
-        r_cat = jnp.concatenate([r_cat, r_cat], axis=1)
+        r_cat = jnp.concatenate([r_hi, r_lo], axis=1)
+        r_cat = jnp.concatenate([r_cat, r_cat], axis=0)
         step = anc // 2
         for m in range(2):
             for k in range(step * m, step * (m + 1)):
                 t_hi, t_lo = split(q[k : k + 1, :] * t)
                 tbuf[traits * k : traits * (k + 1), 0:width] = t_hi
-                tbuf[traits * k : traits * (k + 1), width:] = t_lo
+                tbuf[traits * k : traits * (k + 1), width : 2 * width] = t_lo
             at = slice(traits * step * m, traits * step * (m + 1))
-            acc_sc[at, :] += dot_lanes(tbuf[at, :], r_cat)
+            o = dot(tbuf[at, 0 : 2 * width], r_cat)
+            acc_sc[at, :] += o[:, 0:mv] + o[:, mv:]
         y_hi, y_lo = split(q * q)
         none = jnp.zeros_like(y_hi)
-        acc_in[...] += dot_lanes(
-            jnp.concatenate([y_hi, y_lo], axis=0), jnp.concatenate([s_hi, s_lo], axis=0)
+        acc_in[...] += dot(
+            jnp.concatenate([y_hi, y_lo], axis=0), jnp.concatenate([s_hi, s_lo], axis=1)
         )
 
     def copy(src, dst, send, recv, peer):
@@ -235,19 +245,19 @@
     def outward(t):
         return copy(go.at[t], go.at[t], z_s, z_r.at[t], beside)
 
-    def x_gather(c, j):
-        return copy(go.at[c * sub + j], gp.at[c * sub + j], xa_s, xa_r.at[c], partner)
+    def x_gather(t):
+        return copy(go.at[t], gp.at[t], xa_s, xa_r.at[t // per], partner)
 
     def x_gathered(c):
-        at = pl.ds(c * sub, sub)
+        at = pl.ds(c * per, per)
         return copy(go.at[at], gp.at[at], xa_s, xa_r.at[c], partner)
 
     def put(ref, c, g):
         for j in range(sub):
             ref[c * sub + j] = g[:, 128 * j : 128 * (j + 1)]
 
-    def take(ref, c):
-        return jnp.concatenate([ref[c * sub + j] for j in range(sub)], axis=1)
+    def take(ref, at, count):
+        return jnp.concatenate([ref[at + j] for j in range(count)], axis=1)
 
     for item in first_loads:
         item.wait()
@@ -286,7 +296,7 @@
         exchange(t).wait_recv()
         go[t] = zs[t] + mr[t]
         outward(t).start()
-        x_gather(c, j).start()
+        x_gather(t).start()
 
     def step_near(c, carry):
         put(zs, c, first_pass(lanes(x, c)))
@@ -299,9 +309,9 @@
             def _(t=t):
                 inward(t).start()
 
-            @pl.when(jnp.logical_and(middle, c >= LAG))
+            @pl.when(jnp.logical_and(middle, c >= NEAR_LAG))
             def _(t=t):
-                add_inward(t - LAG * sub)
+                add_inward(t - NEAR_LAG * sub)
 
         return carry
 
@@ -331,34 +341,34 @@
                 add_exchange(c, j)
             return carry
 
-        lax.fori_loop(max(0, chunks - LAG) * sub, min(LAG, chunks) * sub, step_inward, 0)
+        lax.fori_loop(max(0, chunks - NEAR_LAG) * sub, min(LAG, chunks) * sub, step_inward, 0)
         lax.fori_loop(0, chunks, step_exchange, 0)
 
     resid_load.wait()
 
     def step_own(c, carry):
-        for j in range(sub):
-            t = c * sub + j
+        for j in range(own_per):
+            t = c * own_per + j
 
             @pl.when(end)
-            def _(t=t, j=j):
+            def _(t=t):
                 outward(t).wait_recv()
-                x_gather(c, j).start()
-
-        second_pass(lanes(x, c), take(go, c))
+                x_gather(t).start()
+
+        second_pass(pl.multiple_of(x * half + c * own_per * 128, 128), take(go, c * own_per, own_per))
         return carry
 
-    lax.fori_loop(0, chunks, step_own, 0)
+    lax.fori_loop(0, chunks * sub // own_per, step_own, 0)
 
     def step_other(c, carry):
         x_gathered(c).wait_recv()
-        second_pass(lanes(1 - x, c), take(gp, c))
+        second_pass(pl.multiple_of((1 - x) * half + c * per * 128, 128), take(gp, c * per, per))
         return carry
 
-    lax.fori_loop(0, chunks, step_other, 0)
+    lax.fori_loop(0, chunks * sub // per, step_other, 0)
 
     tiles = anc * traits
-    ss[0:tiles, :] = acc_sc[:, 0:mv] + acc_sc[:, mv:]
+    ss[0:tiles, :] = acc_sc[...]
     info = acc_in[0:anc, :] + acc_in[anc:, :]
     ss[tiles:, :] = info[:, 0:mv] + info[:, mv:]
     score_copy = copy(ss, sr, s_s, s_r, twin)
@@ -444,8 +454,10 @@
     tiles = half // 128
     chunks = max(n for n in range(1, MOST + 1) if tiles % n == 0)
     width = half // chunks
+    own_per = max(n for n in range(1, OWN + 1) if tiles % n == 0)
+    per = max(n for n in range(1, OTHER + 1) if tiles % n == 0)
     share = samples // var_n
-    dims = (chunks, width, half, mv * var_n, samples * lax.axis_size("smp"), share, var_n)
+    dims = (chunks, width, half, own_per, per, mv * var_n, samples * lax.axis_size("smp"), share, var_n)
     vmem = pl.BlockSpec(memory_space=pltpu.VMEM)
     dma = pltpu.SemaphoreType.DMA
     part = pltpu.VMEM((half // 128, anc, 128), F32)
@@ -466,22 +478,22 @@
             pltpu.VMEM((anc, samples), jnp.int32),
             pltpu.VMEM((traits, samples), jnp.int32),
             pltpu.VMEM((anc, mv), F32),
-            pltpu.VMEM((mv, samples), BF16),
+            pltpu.VMEM((4 * anc, mv), BF16),
             pltpu.VMEM((anc, samples), F32),
             pltpu.VMEM((anc, samples), F32),
             pltpu.VMEM((mv, 4 * anc), BF16),
             pltpu.VMEM((2 * anc, 2 * mv), BF16),
             pltpu.VMEM((4 * mv, width), BF16),
-            pltpu.VMEM((anc * traits, 2 * width), BF16),
+            pltpu.VMEM((anc * traits, 256 * max(own_per, per)), BF16),
             pltpu.VMEM((4 * mv, 128), F32),
-            pltpu.VMEM((anc * traits, 2 * mv), F32),
+            pltpu.VMEM((anc * traits, mv), F32),
             pltpu.VMEM((2 * anc, 2 * mv), F32),
             part, part, part, part, part, part, part,
             pltpu.VMEM((2 * anc, mv), F32),
             pltpu.VMEM((2 * anc, mv), F32),
             pltpu.VMEM((anc * traits + anc, mv), F32),
             pltpu.VMEM((anc * traits + anc, mv), F32),
-            dma, flags, dma, flags, dma, flags, dma, dma((chunks,)),
+            dma, flags, dma, flags, dma, flags, dma, dma((tiles // per,)),
             dma, dma, dma, dma, dma((8,)),
         ],
         compiler_params=pltpu.CompilerParams(collective_id=0, has_side_effects=True, vmem_limit_bytes=LIMIT),

time: 27.9 us -> 27.7 us (level)
  Pallas kernels: 27.1 us -> 26.8 us
where the time goes in v3:
time: 27.7 us; the launch traced here: 27.4 us
  Pallas kernels  26.8 us (97%)
  between operations  0.64 us (2%)
    pallas_call x1, Pallas kernels, shards(): pl.pallas_call(functools.partial(kernel, dims), out_shape=(pltpu.VMEM((an...  26 us
    pallas_call x1, Pallas kernels, store(): pl.pallas_call(store_kernel, out_shape=tuple((jax.ShapeDtypeStruct(a.shap...  0.8 us

profile of v3, /device:TPU:0, one launch (start us, length us, event | category | flops | bytes accessed | tf_op | source)
XLA Modules:
  0.0 27.4 jit_solution(5754557288475692680)
XLA Ops:
  0.6 26.0 %em_step.1 = (f32[32,480]{1,0:T(8,128)S(1)}, f32[32,480]{1,0:T(8,128)S(1)}, f32[32,128]{1,0:T(8,128)S(1)}, f32[32,128]{1,0:T(8,128)S(1)}, f32[512,128]{1,0:T(8,128)S(1)}) custom-call(bf16[3840,128]{1,0:T(8,128)(2,1)} %geno_in.1, s32[32,3840]{1,0:T(8,128)} %bitcast.5, s32[16,3840]{1,0:T(8,128)} %bitcast.6, f32[32,128]{1,0:T(8,128)} %freqs_in.1), custom_call_target="tpu_custom_call" | custom-call | tf_op jit(solution)/shard_map/em_step/pallas_call | solution.py:465
  26.6 0.8 %store.1 = (f32[32,480]{1,0:T(8,128)}, f32[32,480]{1,0:T(8,128)}, f32[32,128]{1,0:T(8,128)}, f32[32,128]{1,0:T(8,128)}, f32[512,128]{1,0:T(8,128)}) custom-call(f32[32,480]{1,0:T(8,128)S(1)} %get-tuple-element.15.refs_0_, f32[32,480]{1,0:T(8,128)S(1)} %get-tuple-element.16.refs_1_, f32[32,128]{1,0:T(8,128)S(1)} %get-tuple-element.17.refs_2_, ...), custom_call_target="tpu_custom_call" | custom-call | tf_op jit(solution)/shard_map/store/pallas_call | solution.py:421

commit v4 on v3

--- a/solution.py
+++ b/solution.py
@@ -341,8 +341,10 @@
                 add_exchange(c, j)
             return carry
 
-        lax.fori_loop(max(0, chunks - NEAR_LAG) * sub, min(LAG, chunks) * sub, step_inward, 0)
-        lax.fori_loop(0, chunks, step_exchange, 0)
+        for t in range(max(0, chunks - NEAR_LAG) * sub, min(LAG, chunks) * sub):
+            step_inward(t, 0)
+        for c in range(chunks):
+            step_exchange(c, 0)
 
     resid_load.wait()
 

time: 27.7 us -> 27.7 us (level)
  no operation moved by 1% of the time
where the time goes in v4:
time: 27.7 us; the launch traced here: 27.4 us
  Pallas kernels  26.8 us (97%)
  between operations  0.64 us (2%)
    pallas_call x1, Pallas kernels, shards(): pl.pallas_call(functools.partial(kernel, dims), out_shape=(pltpu.VMEM((an...  26 us
    pallas_call x1, Pallas kernels, store(): pl.pallas_call(store_kernel, out_shape=tuple((jax.ShapeDtypeStruct(a.shap...  0.8 us

profile of v4, /device:TPU:0, one launch (start us, length us, event | category | flops | bytes accessed | tf_op | source)
XLA Modules:
  0.0 27.4 jit_solution(12258246993888666483)
XLA Ops:
  0.6 26.0 %em_step.1 = (f32[32,480]{1,0:T(8,128)S(1)}, f32[32,480]{1,0:T(8,128)S(1)}, f32[32,128]{1,0:T(8,128)S(1)}, f32[32,128]{1,0:T(8,128)S(1)}, f32[512,128]{1,0:T(8,128)S(1)}) custom-call(bf16[3840,128]{1,0:T(8,128)(2,1)} %geno_in.1, s32[32,3840]{1,0:T(8,128)} %bitcast.5, s32[16,3840]{1,0:T(8,128)} %bitcast.6, f32[32,128]{1,0:T(8,128)} %freqs_in.1), custom_call_target="tpu_custom_call" | custom-call | tf_op jit(solution)/shard_map/em_step/pallas_call | solution.py:467
  26.6 0.8 %store.1 = (f32[32,480]{1,0:T(8,128)}, f32[32,480]{1,0:T(8,128)}, f32[32,128]{1,0:T(8,128)}, f32[32,128]{1,0:T(8,128)}, f32[512,128]{1,0:T(8,128)}) custom-call(f32[32,480]{1,0:T(8,128)S(1)} %get-tuple-element.15.refs_0_, f32[32,480]{1,0:T(8,128)S(1)} %get-tuple-element.16.refs_1_, f32[32,128]{1,0:T(8,128)S(1)} %get-tuple-element.17.refs_2_, ...), custom_call_target="tpu_custom_call" | custom-call | tf_op jit(solution)/shard_map/store/pallas_call | solution.py:423

commit v5 on v4

--- a/solution.py
+++ b/solution.py
@@ -14,8 +14,6 @@
 LIMIT = 67043328 - 491520
 MOST = 5
 NEAR_LAG = 3
-OWN = 3
-OTHER = 5
 LAG = 3
 
 
@@ -96,7 +94,7 @@
     xs, xr, zs, er, mr, go, gp, fs, fr, ss, sr,
     xs_s, xs_r, z_s, z_r, m_s, m_r, xa_s, xa_r, f_s, f_r, s_s, s_r, in_s,
 ):
-    chunks, width, half, own_per, per, variant_count, sample_count, share, var_n = dims
+    chunks, width, half, parts, variant_count, sample_count, share, var_n = dims
     sub = width // 128
     anc = freqs.shape[0]
     traits = resid.shape[0]
@@ -245,12 +243,15 @@
     def outward(t):
         return copy(go.at[t], go.at[t], z_s, z_r.at[t], beside)
 
+    def part_of(t):
+        return sum(jnp.int32(t >= at) for at, _ in parts[1:])
+
     def x_gather(t):
-        return copy(go.at[t], gp.at[t], xa_s, xa_r.at[t // per], partner)
-
-    def x_gathered(c):
-        at = pl.ds(c * per, per)
-        return copy(go.at[at], gp.at[at], xa_s, xa_r.at[c], partner)
+        return copy(go.at[t], gp.at[t], xa_s, xa_r.at[part_of(t)], partner)
+
+    def x_gathered(n):
+        at = pl.ds(*parts[n])
+        return copy(go.at[at], gp.at[at], xa_s, xa_r.at[n], partner)
 
     def put(ref, c, g):
         for j in range(sub):
@@ -349,25 +350,22 @@
     resid_load.wait()
 
     def step_own(c, carry):
-        for j in range(own_per):
-            t = c * own_per + j
+        for j in range(sub):
+            t = c * sub + j
 
             @pl.when(end)
             def _(t=t):
                 outward(t).wait_recv()
                 x_gather(t).start()
 
-        second_pass(pl.multiple_of(x * half + c * own_per * 128, 128), take(go, c * own_per, own_per))
+        second_pass(pl.multiple_of(x * half + c * sub * 128, 128), take(go, c * sub, sub))
         return carry
 
-    lax.fori_loop(0, chunks * sub // own_per, step_own, 0)
-
-    def step_other(c, carry):
-        x_gathered(c).wait_recv()
-        second_pass(pl.multiple_of((1 - x) * half + c * per * 128, 128), take(gp, c * per, per))
-        return carry
-
-    lax.fori_loop(0, chunks * sub // per, step_other, 0)
+    lax.fori_loop(0, chunks * sub // sub, step_own, 0)
+
+    for n, (at, count) in enumerate(parts):
+        x_gathered(n).wait_recv()
+        second_pass(pl.multiple_of((1 - x) * half + at * 128, 128), take(gp, at, count))
 
     tiles = anc * traits
     ss[0:tiles, :] = acc_sc[...]
@@ -429,6 +427,14 @@
         compiler_params=pltpu.CompilerParams(vmem_limit_bytes=1024 * 1024),
         name="store",
     )(*arrays)
+
+
+def split_tiles(tiles):
+    sizes = [MOST] * max(0, (tiles - 1) // MOST)
+    rest = tiles - sum(sizes)
+    sizes += [size for size in (rest - rest // 2, rest // 2) if size]
+    starts = [sum(sizes[:i]) for i in range(len(sizes))]
+    return tuple(zip(starts, sizes))
 
 
 def fits(genotypes, residuals, freqs, var_n):
@@ -456,10 +462,9 @@
     tiles = half // 128
     chunks = max(n for n in range(1, MOST + 1) if tiles % n == 0)
     width = half // chunks
-    own_per = max(n for n in range(1, OWN + 1) if tiles % n == 0)
-    per = max(n for n in range(1, OTHER + 1) if tiles % n == 0)
+    parts = split_tiles(tiles)
     share = samples // var_n
-    dims = (chunks, width, half, own_per, per, mv * var_n, samples * lax.axis_size("smp"), share, var_n)
+    dims = (chunks, width, half, parts, mv * var_n, samples * lax.axis_size("smp"), share, var_n)
     vmem = pl.BlockSpec(memory_space=pltpu.VMEM)
     dma = pltpu.SemaphoreType.DMA
     part = pltpu.VMEM((half // 128, anc, 128), F32)
@@ -486,7 +491,7 @@
             pltpu.VMEM((mv, 4 * anc), BF16),
             pltpu.VMEM((2 * anc, 2 * mv), BF16),
             pltpu.VMEM((4 * mv, width), BF16),
-            pltpu.VMEM((anc * traits, 256 * max(own_per, per)), BF16),
+            pltpu.VMEM((anc * traits, 256 * max(width // 128, MOST)), BF16),
             pltpu.VMEM((4 * mv, 128), F32),
             pltpu.VMEM((anc * traits, mv), F32),
             pltpu.VMEM((2 * anc, 2 * mv), F32),
@@ -495,7 +500,7 @@
             pltpu.VMEM((2 * anc, mv), F32),
             pltpu.VMEM((anc * traits + anc, mv), F32),
             pltpu.VMEM((anc * traits + anc, mv), F32),
-            dma, flags, dma, flags, dma, flags, dma, dma((tiles // per,)),
+            dma, flags, dma, flags, dma, flags, dma, dma((len(parts),)),
             dma, dma, dma, dma, dma((8,)),
         ],
         compiler_params=pltpu.CompilerParams(collective_id=0, has_side_effects=True, vmem_limit_bytes=LIMIT),

time: 27.7 us -> 27.8 us (level)
  no operation moved by 1% of the time
where the time goes in v5:
time: 27.8 us; the launch traced here: 27.6 us
  Pallas kernels  26.9 us (97%)
  between operations  0.64 us (2%)
    pallas_call x1, Pallas kernels, shards(): pl.pallas_call(functools.partial(kernel, dims), out_shape=(pltpu.VMEM((an...  26.1 us
    pallas_call x1, Pallas kernels, store(): pl.pallas_call(store_kernel, out_shape=tuple((jax.ShapeDtypeStruct(a.shap...  0.8 us

profile of v5, /device:TPU:0, one launch (start us, length us, event | category | flops | bytes accessed | tf_op | source)
XLA Modules:
  0.0 27.6 jit_solution(17545145595518096276)
XLA Ops:
  0.6 26.1 %em_step.1 = (f32[32,480]{1,0:T(8,128)S(1)}, f32[32,480]{1,0:T(8,128)S(1)}, f32[32,128]{1,0:T(8,128)S(1)}, f32[32,128]{1,0:T(8,128)S(1)}, f32[512,128]{1,0:T(8,128)S(1)}) custom-call(bf16[3840,128]{1,0:T(8,128)(2,1)} %geno_in.1, s32[32,3840]{1,0:T(8,128)} %bitcast.5, s32[16,3840]{1,0:T(8,128)} %bitcast.6, f32[32,128]{1,0:T(8,128)} %freqs_in.1), custom_call_target="tpu_custom_call" | custom-call | tf_op jit(solution)/shard_map/em_step/pallas_call | solution.py:472
  26.8 0.8 %store.1 = (f32[32,480]{1,0:T(8,128)}, f32[32,480]{1,0:T(8,128)}, f32[32,128]{1,0:T(8,128)}, f32[32,128]{1,0:T(8,128)}, f32[512,128]{1,0:T(8,128)}) custom-call(f32[32,480]{1,0:T(8,128)S(1)} %get-tuple-element.15.refs_0_, f32[32,480]{1,0:T(8,128)S(1)} %get-tuple-element.16.refs_1_, f32[32,128]{1,0:T(8,128)S(1)} %get-tuple-element.17.refs_2_, ...), custom_call_target="tpu_custom_call" | custom-call | tf_op jit(solution)/shard_map/store/pallas_call | solution.py:421

commit v6 on v3

--- a/solution.py
+++ b/solution.py
@@ -13,7 +13,7 @@
 BF16 = jnp.bfloat16
 LIMIT = 67043328 - 491520
 MOST = 5
-NEAR_LAG = 3
+NEAR_LAG = 2
 OWN = 3
 OTHER = 5
 LAG = 3

time: 27.7 us -> 27.7 us (level)
  no operation moved by 1% of the time
where the time goes in v6:
time: 27.7 us; the launch traced here: 27.5 us
  Pallas kernels  26.9 us (97%)
  between operations  0.64 us (2%)
    pallas_call x1, Pallas kernels, shards(): pl.pallas_call(functools.partial(kernel, dims), out_shape=(pltpu.VMEM((an...  26.1 us
    pallas_call x1, Pallas kernels, store(): pl.pallas_call(store_kernel, out_shape=tuple((jax.ShapeDtypeStruct(a.shap...  0.8 us

profile of v6, /device:TPU:0, one launch (start us, length us, event | category | flops | bytes accessed | tf_op | source)
XLA Modules:
  0.0 27.5 jit_solution(12301495080518638461)
XLA Ops:
  0.6 26.1 %em_step.1 = (f32[32,480]{1,0:T(8,128)S(1)}, f32[32,480]{1,0:T(8,128)S(1)}, f32[32,128]{1,0:T(8,128)S(1)}, f32[32,128]{1,0:T(8,128)S(1)}, f32[512,128]{1,0:T(8,128)S(1)}) custom-call(bf16[3840,128]{1,0:T(8,128)(2,1)} %geno_in.1, s32[32,3840]{1,0:T(8,128)} %bitcast.5, s32[16,3840]{1,0:T(8,128)} %bitcast.6, f32[32,128]{1,0:T(8,128)} %freqs_in.1), custom_call_target="tpu_custom_call" | custom-call | tf_op jit(solution)/shard_map/em_step/pallas_call | solution.py:465
  26.7 0.8 %store.1 = (f32[32,480]{1,0:T(8,128)}, f32[32,480]{1,0:T(8,128)}, f32[32,128]{1,0:T(8,128)}, f32[32,128]{1,0:T(8,128)}, f32[512,128]{1,0:T(8,128)}) custom-call(f32[32,480]{1,0:T(8,128)S(1)} %get-tuple-element.15.refs_0_, f32[32,480]{1,0:T(8,128)S(1)} %get-tuple-element.16.refs_1_, f32[32,128]{1,0:T(8,128)S(1)} %get-tuple-element.17.refs_2_, ...), custom_call_target="tpu_custom_call" | custom-call | tf_op jit(solution)/shard_map/store/pallas_call | solution.py:421
